TPU v7x, 32 devices: a whole 2x2x4 slice. The times are simulated.
32 devices in a mesh: dp: 8 (over z, y), tensor: 4 (over x, core).
Axes of the slice: x: 2, y: 2, z: 4, core: 2. Of those that a mesh axis runs over, the one named last changes fastest.
Arguments:
- hidden: bfloat16 [2048, 18432], P('dp', 'tensor'), may hold values from -6 to 6
- down_weight: bfloat16 [18432, 4608], P('tensor', 'dp'), may hold values from -0.046875 to 0.046875
- residual: bfloat16 [2048, 4608], P('dp'), may hold values from -6 to 6
- post_gain: float32 [4608], replicated, may hold values from 0.5 to 1.5
- pre_gain: float32 [4608], replicated, may hold values from 0.5 to 1.5
- cast_scale: float32 [1], replicated, may hold values from 100 to 400
- amax_history: float32 [3, 1024], replicated, may hold values from 0.25 to 4
Outputs:
- cast_out: bfloat16 [2048, 4608], P('dp')
- residual_out: bfloat16 [2048, 4608], P('dp')
- peaks: float32 [3], replicated
- new_history: float32 [3, 1024], replicated
- new_scales: float32 [3], replicated
All inputs are finite; a program needn't handle non-finite values.
Results may differ from a plain program's by a relative error of at most 0.012.
Values may be sent and summed in bfloat16 or wider, within the bound.
A program may use at most 128 MiB of HBM per device.

v0:
```python
import jax
import jax.numpy as jnp
from jax import lax
from jax.sharding import PartitionSpec as P

norm_epsilon = 1e-06
float_limit = 448.0


def rms_norm(values, gain_vector):
    return (
        values
        * lax.rsqrt(jnp.mean(values * values, axis=-1, keepdims=True) + norm_epsilon)
        * gain_vector
    )


def finish(summed, stream_in, post_gain, pre_gain, stale_scale):
    stream = stream_in.astype(jnp.float32) + rms_norm(summed, post_gain)
    normed = rms_norm(stream, pre_gain)
    cast_rows = (jnp.clip(normed * stale_scale, -float_limit, float_limit) / stale_scale).astype(
        jnp.bfloat16
    )
    peak_values = jnp.stack(
        [jnp.max(jnp.abs(summed)), jnp.max(jnp.abs(stream)), jnp.max(jnp.abs(normed))]
    )
    return (cast_rows, stream.astype(jnp.bfloat16), peak_values)


def on_device(hidden, down_weight, residual, post_gain, pre_gain, cast_scale, amax_history):
    stale_scale = cast_scale[0]
    partial_value = jnp.dot(
        lax.all_gather(hidden, "dp", axis=0, tiled=True),
        down_weight,
        preferred_element_type=jnp.float32,
    )
    column_total = lax.psum(partial_value.astype(jnp.bfloat16), "tensor").astype(jnp.float32)
    summed = lax.all_to_all(
        column_total.astype(jnp.bfloat16), "dp", split_axis=0, concat_axis=1, tiled=True
    ).astype(column_total.dtype)
    cast_out, residual_out, peak_values = finish(summed, residual, post_gain, pre_gain, stale_scale)
    peak_values = lax.pmax(peak_values, ("dp", "tensor"))
    new_history = jnp.concatenate([peak_values[:, None], amax_history[:, :-1]], axis=1)
    new_scales = float_limit / jnp.maximum(jnp.max(new_history, axis=1), 1.0)
    return (cast_out, residual_out, peak_values, new_history, new_scales)


def solution(mesh):
    in_specs = (P("dp", "tensor"), P("tensor", "dp"), P("dp", None), P(), P(), P(), P())
    out_specs = (P("dp", None), P("dp", None), P(), P(), P())
    return jax.shard_map(
        on_device, mesh=mesh, in_specs=in_specs, out_specs=out_specs, check_vma=False
    )
```

profile of v0, /device:TPU:10, one launch (start us, length us, event | category | flops | bytes accessed | tf_op | source)
XLA Modules:
  0.0 571.8 jit_solution(3271551437250830169)
XLA Ops:
  7.2 0.0 all-gather.2.cloned.1.call-start
  7.2 0.7 all-gather.2.cloned.1.call-update
  7.9 0.0 all-reduce.2.cloned.1.call-start
  7.9 365.1 %all-gather.2.cloned.1.call-done = bf16[2048,4608]{1,0:T(8,128)(2,1)} async-done(((bf16[256,4608]{1,0:T(8,128)(2,1)}), bf16[2048,4608]{1,0:T(8,128)(2,1)}) %all-gather.2.cloned.1.call-update) | async-done | bytes 18874384 | tf_op jit(solution)/shard_map/all_gather | solution.py:33
  373.0 16.5 %convolution_convert_fusion = bf16[2048,576]{0,1:T(8,128)(2,1)S(1)} fusion(bf16[2048,4608]{1,0:T(8,128)(2,1)} %all-gather.2.cloned.1.call-done, bf16[4608,576]{0,1:T(8,128)(2,1)} %param.8), kind=kOutput, calls=%fused_computation.10 | convolution fusion | flops 10872815616 | bytes 26542080 | tf_op jit(solution)/shard_map/dot_general | solution.py:32
  389.6 1.6 copy.21
  391.2 0.0 all-reduce.2.cloned.1.call-update
  391.2 55.0 %all-reduce.2.cloned.1.call-done = bf16[8,256,576]{1,2,0:T(8,128)(2,1)} async-done(((bf16[8,256,576]{1,2,0:T(8,128)(2,1)}), bf16[8,256,576]{1,2,0:T(8,128)(2,1)}) %all-reduce.2.cloned.1.call-update) | async-done | bytes 2359312 | tf_op jit(solution)/shard_map/psum | solution.py:37
  446.1 6.1 %all-to-all-start = ((bf16[8,256,576]{1,2,0:T(8,128)(2,1)}), bf16[8,256,576]{1,2,0:T(8,128)(2,1)S(1)}, u32[]{:S(2)}, u32[]{:S(2)}) async-start(bf16[8,256,576]{1,2,0:T(8,128)(2,1)} %all-reduce.2.cloned.1.call-done), calls=%async_computation | async-start | bytes 4718592 | tf_op jit(solution)/shard_map/all_to_all | solution.py:38
  452.2 0.0 copy-start.2
  452.2 4.3 copy.14
  456.5 0.0 copy-start.3
  457.1 46.4 %all-to-all-done = bf16[8,256,576]{1,2,0:T(8,128)(2,1)S(1)} async-done(((bf16[8,256,576]{1,2,0:T(8,128)(2,1)}), bf16[8,256,576]{1,2,0:T(8,128)(2,1)S(1)}, u32[]{:S(2)}, u32[]{:S(2)}) %all-to-all-start) | async-done | bytes 2359328 | tf_op jit(solution)/shard_map/all_to_all | solution.py:38
  503.5 0.0 copy-start
  503.5 1.2 abs_reduce_fusion.2
  504.7 0.0 copy-done.2
  504.7 3.3 multiply_reduce_fusion
  508.0 0.0 copy-done.3
  508.0 0.0 copy-done
  508.0 0.0 copy-start.4
  508.1 4.8 abs_reduce_fusion.1
  512.8 0.0 copy-start.1
  512.8 2.2 pad_maximum_fusion.1
  515.0 0.0 copy-done.4
  515.0 0.1 slice_reduce_fusion
  515.1 41.9 %pmax.7 = f32[3]{0:T(128)S(1)} all-reduce(f32[3]{0:T(128)S(1)} %pad_maximum_fusion.1), channel_id=1, replica_groups=mesh['dp'=8,'tensor'=4] {'dp','tensor'}, use_global_device_ids=true, to_apply=%region_6.7 | all-reduce | flops 3 | bytes 24 | tf_op jit(solution)/shard_map/pmax | solution.py:42
  557.0 0.0 copy-start.5
  557.0 0.1 copy.16
  557.1 0.5 maximum_divide_fusion
  557.6 4.3 copy.17
  561.9 0.0 copy-done.1
  561.9 2.4 copy.18
  564.3 0.0 copy-done.5
  564.3 0.7 pad_maximum_fusion
  (2 shorter events, 0.0 us)
Async XLA Ops:
  7.2 365.9 %all-gather.2.cloned.1.call-start = ((), (), s32[]{:S(2)}) async-start(), calls=%async_computation.1 | async-start | bytes 21233664 | tf_op jit(solution)/shard_map/all_gather | solution.py:33
  7.9 438.2 %all-reduce.2.cloned.1.call-start = ((), (), s32[]{:S(2)}) async-start(), calls=%async_computation.2 | async-start | bytes 4718592 | tf_op jit(solution)/shard_map/psum | solution.py:37
  446.1 57.4 %all-to-all-start = ((bf16[8,256,576]{1,2,0:T(8,128)(2,1)}), bf16[8,256,576]{1,2,0:T(8,128)(2,1)S(1)}, u32[]{:S(2)}, u32[]{:S(2)}) async-start(bf16[8,256,576]{1,2,0:T(8,128)(2,1)} %all-reduce.2.cloned.1.call-done), calls=%async_computation | async-start | bytes 4718592 | tf_op jit(solution)/shard_map/all_to_all | solution.py:38
  452.2 52.5 %copy-start.2 = (f32[4608]{0:T(1024)S(1)}, f32[4608]{0:T(1024)}, u32[]{:S(2)}) copy-start(f32[4608]{0:T(1024)} %param.10) | copy-start | bytes 55300
  456.5 51.5 %copy-start.3 = (f32[4608]{0:T(1024)S(1)}, f32[4608]{0:T(1024)}, u32[]{:S(2)}) copy-start(f32[4608]{0:T(1024)} %param.11) | copy-start | bytes 55300
  503.5 4.5 copy-start
  508.0 7.0 %copy-start.4 = (f32[3,1024]{1,0:T(4,128)S(1)}, f32[3,1024]{1,0:T(4,128)}, u32[]{:S(2)}) copy-start(f32[3,1024]{1,0:T(4,128)} %param.13) | copy-start | bytes 36868
  512.8 49.0 %copy-start.1 = (bf16[256,4608]{0,1:T(8,128)(2,1)S(1)}, bf16[256,4608]{0,1:T(8,128)(2,1)}, u32[]{:S(2)}) copy-start(bf16[256,4608]{0,1:T(8,128)(2,1)} %get-tuple-element.15) | copy-start | bytes 7077892
  557.0 7.3 %copy-start.5 = (f32[3]{0:T(128)}, f32[3]{0:T(128)S(1)}, u32[]{:S(2)}) copy-start(f32[3]{0:T(128)S(1)} %pmax.7) | copy-start | bytes 40
Sparse Core Ops, SparseCore 0:
  9.5 363.4 all-gather.1
  391.3 54.8 all-reduce.1
where the time goes:
time: 572 us
  waiting for transfers between devices  467 us (82%)
  blocking collectives  41.9 us (7%)
  matrix products  16.5 us (3%)
  between operations  14.7 us (3%)
  other arithmetic  12.8 us (2%)
  local copies, waits for them, and re-layouts  12.6 us (2%)
  starting transfers between devices  6.13 us (1%)
    all_gather x1, waiting for transfers between devices, on_device(): lax.all_gather(hidden, 'dp', axis=0, tiled=True)  365 us
    psum x1, waiting for transfers between devices, on_device(): lax.psum(partial_value.astype(jnp.bfloat16), 'tensor').astype(jnp.float32)  55 us
    all_to_all x1, waiting for transfers between devices, on_device(): lax.all_to_all(column_total.astype(jnp.bfloat16), 'dp', split_axis=0, con...  46.4 us
    pmax x1, blocking collectives, on_device(): peak_values = lax.pmax(peak_values, ('dp', 'tensor'))  41.9 us
    dot_general x1, matrix products, on_device(): jnp.dot(lax.all_gather(hidden, 'dp', axis=0, tiled=True), down_weight, pr...  16.5 us
  transfers between devices with their start and end apart: 3, of which 3 were waited for; matrix products, arithmetic and copies ran while one was open for 1% of the time, Pallas kernels for 0%

commit v1 on v0

--- a/solution.py
+++ b/solution.py
@@ -5,6 +5,11 @@
 
 norm_epsilon = 1e-06
 float_limit = 448.0
+
+
+def summed_here(shard, axis):
+    pieces = lax.all_gather(shard, axis)
+    return jnp.sum(pieces, axis=0)
 
 
 def rms_norm(values, gain_vector):
@@ -34,7 +39,7 @@
         down_weight,
         preferred_element_type=jnp.float32,
     )
-    column_total = lax.psum(partial_value.astype(jnp.bfloat16), "tensor").astype(jnp.float32)
+    column_total = summed_here(partial_value.astype(jnp.bfloat16), "tensor").astype(jnp.float32)
     summed = lax.all_to_all(
         column_total.astype(jnp.bfloat16), "dp", split_axis=0, concat_axis=1, tiled=True
     ).astype(column_total.dtype)

time: 572 us -> 612 us (1.070)
  local copies, waits for them, and re-layouts: 12.6 us -> 28.8 us
  other arithmetic: 12.8 us -> 26.1 us
  waiting for transfers between devices: 467 us -> 476 us
    all_gather x0 -> x1, waiting for transfers between devices: none -> 63.5 us  [summed_here(): pieces = lax.all_gather(shard, axis)]
    psum x1 -> x0, waiting for transfers between devices: 55 us -> none  [on_device(): lax.psum(partial_value.astype(jnp.bfloat16), 'tensor').astype(jnp.float32)]
    all_gather x0 -> x1, local copies, waits for them, and re-layouts: none -> 16.2 us  [summed_here(): pieces = lax.all_gather(shard, axis)]
    reduce_sum x0 -> x1, other arithmetic: none -> 13.2 us  [summed_here(): return jnp.sum(pieces, axis=0)]
where the time goes in v1:
time: 612 us; the launch traced here: 611 us
  waiting for transfers between devices  476 us (78%)
  blocking collectives  41.9 us (7%)
  local copies, waits for them, and re-layouts  28.8 us (5%)
  other arithmetic  26.1 us (4%)
  matrix products  17.5 us (3%)
  between operations  14.7 us (2%)
  starting transfers between devices  6.13 us (1%)
    all_gather x1, waiting for transfers between devices, on_device(): lax.all_gather(hidden, 'dp', axis=0, tiled=True)  365 us
    all_gather x1, waiting for transfers between devices, summed_here(): pieces = lax.all_gather(shard, axis)  63.5 us
    all_to_all x1, waiting for transfers between devices, on_device(): lax.all_to_all(column_total.astype(jnp.bfloat16), 'dp', split_axis=0, con...  46.9 us
    pmax x1, blocking collectives, on_device(): peak_values = lax.pmax(peak_values, ('dp', 'tensor'))  41.9 us
    dot_general x1, matrix products, on_device(): jnp.dot(lax.all_gather(hidden, 'dp', axis=0, tiled=True), down_weight, pr...  17.5 us
    all_gather x1, local copies, waits for them, and re-layouts, summed_here(): pieces = lax.all_gather(shard, axis)  16.2 us
    reduce_sum x1, other arithmetic, summed_here(): return jnp.sum(pieces, axis=0)  13.2 us
  transfers between devices with their start and end apart: 3, of which 3 were waited for; matrix products, arithmetic and copies ran while one was open for 1% of the time, Pallas kernels for 0%

profile of v1, /device:TPU:10, one launch (start us, length us, event | category | flops | bytes accessed | tf_op | source)
XLA Modules:
  0.0 611.4 jit_solution(7275621182953503239)
XLA Ops:
  7.2 0.0 all-gather.4.cloned.1.call-start
  7.2 0.7 all-gather.4.cloned.1.call-update
  7.9 0.0 all-gather.6.cloned.1.call-start
  7.9 365.1 %all-gather.4.cloned.1.call-done = bf16[2048,4608]{1,0:T(8,128)(2,1)} async-done(((bf16[256,4608]{1,0:T(8,128)(2,1)}), bf16[2048,4608]{1,0:T(8,128)(2,1)}) %all-gather.4.cloned.1.call-update) | async-done | bytes 18874384 | tf_op jit(solution)/shard_map/all_gather | solution.py:38
  373.0 17.5 %convolution_convert_fusion = bf16[2048,576]{0,1:T(8,128)(2,1)} fusion(bf16[2048,4608]{1,0:T(8,128)(2,1)} %all-gather.4.cloned.1.call-done, bf16[4608,576]{0,1:T(8,128)(2,1)} %param.8), kind=kOutput, calls=%fused_computation.10 | convolution fusion | flops 10872815616 | bytes 26542080 | tf_op jit(solution)/shard_map/dot_general | solution.py:37
  390.6 0.0 all-gather.6.cloned.1.call-update
  390.6 63.5 %all-gather.6.cloned.1.call-done = bf16[8192,576]{0,1:T(8,128)(2,1)} async-done(((bf16[2048,576]{0,1:T(8,128)(2,1)}), bf16[8192,576]{0,1:T(8,128)(2,1)}) %all-gather.6.cloned.1.call-update) | async-done | bytes 9437200 | tf_op jit(solution)/shard_map/all_gather | solution.py:11
  454.1 16.2 %reshape.36 = bf16[4,2048,576]{1,0,2:T(4,128)(2,1)} reshape(bf16[8192,576]{0,1:T(8,128)(2,1)} %all-gather.6.cloned.1.call-done) | data formatting | bytes 18874368 | tf_op jit(solution)/shard_map/all_gather | solution.py:11
  470.2 13.2 %reduce_sum.30 = bf16[2048,576]{0,1:T(8,128)(2,1)S(1)} reduce(bf16[4,2048,576]{1,0,2:T(4,128)(2,1)} %reshape.36, bf16[]{:T(256)} %constant.4.clone.1), dimensions={0}, to_apply=%region_0.0 | reduce | flops 3538944 | bytes 11796482 | tf_op jit(solution)/shard_map/reduce_sum | solution.py:12
  483.5 1.6 copy.25
  485.0 6.1 all-to-all-start
  491.1 0.0 copy-start.2
  491.1 4.3 copy.18
  495.4 0.0 copy-start.3
  496.0 46.9 %all-to-all-done = bf16[8,256,576]{1,2,0:T(8,128)(2,1)S(1)} async-done(((bf16[8,256,576]{1,2,0:T(8,128)(2,1)}), bf16[8,256,576]{1,2,0:T(8,128)(2,1)S(1)}, u32[]{:S(2)}, u32[]{:S(2)}) %all-to-all-start) | async-done | bytes 2359328 | tf_op jit(solution)/shard_map/all_to_all | solution.py:43
  542.9 0.0 copy-start
  542.9 1.2 abs_reduce_fusion.2
  544.1 0.0 copy-done.2
  544.1 3.3 multiply_reduce_fusion
  547.5 0.0 copy-done.3
  547.5 0.0 copy-done
  547.5 0.0 copy-start.4
  547.5 4.8 abs_reduce_fusion.1
  552.3 0.0 copy-start.1
  552.3 2.2 pad_maximum_fusion.1
  554.5 0.0 copy-done.4
  554.5 0.1 slice_reduce_fusion
  554.6 41.9 %pmax.7 = f32[3]{0:T(128)S(1)} all-reduce(f32[3]{0:T(128)S(1)} %pad_maximum_fusion.1), channel_id=1, replica_groups=mesh['dp'=8,'tensor'=4] {'dp','tensor'}, use_global_device_ids=true, to_apply=%region_6.7 | all-reduce | flops 3 | bytes 24 | tf_op jit(solution)/shard_map/pmax | solution.py:47
  596.5 0.0 copy-start.5
  596.5 0.1 copy.20
  596.6 0.5 maximum_divide_fusion
  597.1 4.3 copy.21
  601.4 0.0 copy-done.1
  601.4 2.4 copy.22
  603.8 0.0 copy-done.5
  603.8 0.7 pad_maximum_fusion
  (2 shorter events, 0.0 us)
Async XLA Ops:
  7.2 365.9 %all-gather.4.cloned.1.call-start = ((), (), s32[]{:S(2)}) async-start(), calls=%async_computation.1 | async-start | bytes 21233664 | tf_op jit(solution)/shard_map/all_gather | solution.py:38
  7.9 446.2 %all-gather.6.cloned.1.call-start = ((), (), s32[]{:S(2)}) async-start(), calls=%async_computation.2 | async-start | bytes 11796480 | tf_op jit(solution)/shard_map/all_gather | solution.py:11
  485.0 57.9 %all-to-all-start = ((bf16[8,256,576]{1,2,0:T(8,128)(2,1)}), bf16[8,256,576]{1,2,0:T(8,128)(2,1)S(1)}, u32[]{:S(2)}, u32[]{:S(2)}) async-start(bf16[8,256,576]{1,2,0:T(8,128)(2,1)} %bitcast.32), calls=%async_computation | async-start | bytes 4718592 | tf_op jit(solution)/shard_map/all_to_all | solution.py:43
  491.1 53.0 %copy-start.2 = (f32[4608]{0:T(1024)S(1)}, f32[4608]{0:T(1024)}, u32[]{:S(2)}) copy-start(f32[4608]{0:T(1024)} %param.10) | copy-start | bytes 55300
  495.4 52.1 %copy-start.3 = (f32[4608]{0:T(1024)S(1)}, f32[4608]{0:T(1024)}, u32[]{:S(2)}) copy-start(f32[4608]{0:T(1024)} %param.11) | copy-start | bytes 55300
  542.9 4.6 copy-start
  547.5 7.0 %copy-start.4 = (f32[3,1024]{1,0:T(4,128)S(1)}, f32[3,1024]{1,0:T(4,128)}, u32[]{:S(2)}) copy-start(f32[3,1024]{1,0:T(4,128)} %param.13) | copy-start | bytes 36868
  552.3 49.1 %copy-start.1 = (bf16[256,4608]{0,1:T(8,128)(2,1)S(1)}, bf16[256,4608]{0,1:T(8,128)(2,1)}, u32[]{:S(2)}) copy-start(bf16[256,4608]{0,1:T(8,128)(2,1)} %get-tuple-element.20) | copy-start | bytes 7077892
  596.5 7.3 %copy-start.5 = (f32[3]{0:T(128)}, f32[3]{0:T(128)S(1)}, u32[]{:S(2)}) copy-start(f32[3]{0:T(128)S(1)} %pmax.7) | copy-start | bytes 40
Sparse Core Ops, SparseCore 0:
  9.5 363.4 all-gather.3
  390.7 63.2 all-gather.5
